TPU v7x, 8 devices: a whole 2x2x1 slice. The times are simulated.
8 devices in a mesh: rep: 2 (over y, z), dp: 4 (over x, core).
Axes of the slice: x: 2, y: 2, z: 1, core: 2. Of those that a mesh axis runs over, the one named last changes fastest.
Arguments:
- x: bfloat16 [8, 2048, 896], P(('rep', 'dp')), parts along dimension 0
- dy: bfloat16 [8, 2048, 896], P(('rep', 'dp')), parts along dimension 0
- w_gate: bfloat16 [2, 896, 2560], replicated
- w_up: bfloat16 [2, 896, 2560], replicated
- w_down: bfloat16 [2, 2560, 896], replicated
- m_w_gate: float32 [2, 896, 2560], replicated
- m_w_up: float32 [2, 896, 2560], replicated
- m_w_down: float32 [2, 2560, 896], replicated
- v_w_gate: float32 [2, 896, 2560], replicated
- v_w_up: float32 [2, 896, 2560], replicated
- v_w_down: float32 [2, 2560, 896], replicated
Outputs:
- output 1: bfloat16 [4, 896, 2560], P('rep'), parts along dimension 0
- output 2: bfloat16 [4, 896, 2560], P('rep'), parts along dimension 0
- output 3: bfloat16 [4, 2560, 896], P('rep'), parts along dimension 0
- output 4: float32 [4, 896, 2560], P('rep'), parts along dimension 0
- output 5: float32 [4, 896, 2560], P('rep'), parts along dimension 0
- output 6: float32 [4, 2560, 896], P('rep'), parts along dimension 0
- output 7: float32 [4, 896, 2560], P('rep'), parts along dimension 0
- output 8: float32 [4, 896, 2560], P('rep'), parts along dimension 0
- output 9: float32 [4, 2560, 896], P('rep'), parts along dimension 0
There are 2 independent parts. A program takes and returns all parts, laid end to end along the dimension named above; an argument that names none is the same for every part.
All inputs are finite; a program needn't handle non-finite values.
Results may differ from a plain program's by a relative error of at most 0.022.
Values are sent between devices in bfloat16 or wider.
A program may use at most 2.5 GiB of HBM per device.

v0:
```python
import functools

import jax
import jax.numpy as jnp
from jax import lax
from jax.experimental import pallas as pl
from jax.experimental.pallas import tpu as pltpu
from jax.sharding import PartitionSpec as P


MESH = pl.DeviceIdType.MESH
F32, BF16 = jnp.float32, jnp.bfloat16
TOKENS, D, FF, LAYERS = 2048, 896, 2560, 2
T = 256
NT = FF // T
TILES = LAYERS * NT
ROWS = 512
HALF, QUARTER = D // 2, D // 4
LAG = 5
PIECES = ((0, 4), (4, 10), (10, 14), (14, 18), (18, 20))
N = len(PIECES)
EARLY = PIECES[0][1]
COUNT = 3 * LAYERS * D * FF
FOLD = [((slice(0, 64), slice(256 * i, 256 * i + 256)), (slice(64 * i, 64 * i + 64), slice(0, 256))) for i in range(3)] + [
    ((slice(32 * i, 32 * i + 32), slice(768, 896)), (slice(192, 224), slice(128 * i, 128 * i + 128))) for i in range(2)
]


def dot(a, b, ca, cb):
    return lax.dot_general(a, b, (((ca,), (cb,)), ((), ())), preferred_element_type=F32)


def normed(h):
    wide = h.astype(F32)
    return (wide * lax.rsqrt(jnp.mean(wide * wide, -1, keepdims=True) + 1e-6)).astype(BF16)


def lanes(sq):
    by_row = jnp.sum(sq.reshape(sq.shape[0] // 8, 8, sq.shape[1]), axis=0)
    return sum(by_row[:, i * 128 : (i + 1) * 128] for i in range(sq.shape[1] // 128))


def grads_kernel(
    x_hbm, dy_hbm, wg, wu, wd,
    *refs,
):
    own, sibling, other = refs[:3]
    pieces = refs[2 : 2 + N]
    (
    factor,
    x, h, dy, a, acc, hs, dgs, dus,
    mine_gu, mine_d, r1_gu, r1_d, xs, xk, r2, squares, ss_all,
    in_sem, d_send, d_recv, x_send, x_recv, out_sem, g_send, g_recv, e_send, e_recv, s_send, s_recv,
    ) = refs[2 + N :]
    s = pl.program_id(0)
    me, rep = lax.axis_index("dp"), lax.axis_index("rep")
    core, chip = lax.rem(me, 2), lax.div(me, 2)
    partner, across = me + 1 - 2 * core, lax.rem(me + 2, 4)
    t = s - NT

    def rows_loop(body, first=0, last=TOKENS):
        for i in range(first, last, ROWS):
            body(pl.ds(i, ROWS))

    def to_partner(t):
        slot = lax.rem(t, 2)
        theirs = pl.ds(pl.multiple_of((1 - core) * HALF, 64), HALF)
        theirs_d = pl.ds(pl.multiple_of((1 - core) * (T // 2), 64), T // 2)
        make = functools.partial(pltpu.make_async_remote_copy, device_id=(rep, partner), device_id_type=MESH)
        return (
            make(mine_gu.at[slot, :, theirs, :], r1_gu.at[slot], d_send.at[slot, 0], d_recv.at[slot, 0]),
            make(mine_d.at[slot, theirs_d, :], r1_d.at[slot], d_send.at[slot, 1], d_recv.at[slot, 1]),
        )

    def to_across(t):
        slot = lax.rem(t, LAG + 1)
        make = functools.partial(pltpu.make_async_remote_copy, device_id=(rep, across), device_id_type=MESH)
        return (make(xs.at[slot], r2.at[t + LAG], x_send.at[slot], x_recv.at[t]),)

    def outs(t, piece):
        first, src = PIECES[piece][0], r2.at[t + LAG]
        everywhere = pl.ds(pl.multiple_of(t * T, T), T)
        here = pl.ds(pl.multiple_of((t - first) * T, T), T)
        make = functools.partial(pltpu.make_async_remote_copy, device_id_type=MESH)
        copies = [
            pltpu.make_async_copy(src, own.at[:, :, everywhere], out_sem.at[t, 0]),
            make(src, sibling.at[:, :, everywhere], g_send.at[t], g_recv.at[t], device_id=(rep, partner)),
        ]
        if piece:
            copies.append(pltpu.make_async_copy(src, pieces[piece].at[:, :, here], out_sem.at[t, 1]))
        else:
            copies.append(make(src, other.at[:, :, here], e_send.at[t], e_recv.at[t], device_id=(rep, across)))
        return copies

    def chip_sum(t):
        slot, xslot = lax.rem(t + 2, 2), lax.rem(t + LAG + 1, LAG + 1)
        for keep in (True, False):
            q = chip if keep else 1 - chip
            mine = pl.ds(pl.multiple_of(core * HALF + q * QUARTER, 32), QUARTER)
            got = pl.ds(pl.multiple_of(q * QUARTER, 32), QUARTER)
            mine_rows = pl.ds(pl.multiple_of(core * (T // 2) + q * (T // 4), 64), T // 4)
            got_rows = pl.ds(pl.multiple_of(q * (T // 4), 64), T // 4)
            to = xk if keep else xs
            for i in range(2):
                total = mine_gu[slot, i, mine, :].astype(F32) + r1_gu[slot, i, got, :].astype(F32)
                to[xslot, i] = total.astype(to.dtype)
            total = (mine_d[slot, mine_rows, :].astype(F32) + r1_d[slot, got_rows, :].astype(F32)).astype(to.dtype)
            for (rows, cols), (at_rows, at_cols) in FOLD:
                to[xslot, 2, at_rows, at_cols] = total[rows, cols]

    def finish(t):
        xslot = lax.rem(t + LAG + 1, LAG + 1)
        part = squares[...]
        for i in range(3):
            g = (xk[xslot, i] + r2[t + LAG, i].astype(F32)).astype(BF16)
            r2[t + LAG, i] = g
            g = g.astype(F32)
            part += lanes(g * g)
        squares[...] = jnp.where(t >= 0, part, squares[...])

    def put_out(t):
        for piece, (first, last) in enumerate(PIECES):

            @pl.when((t >= first) & (t < last))
            def _():
                for c in outs(t, piece):
                    c.start()

    @pl.when(s == 0)
    def _():
        barrier = pltpu.get_barrier_semaphore()
        for k in range(1, 4):
            pl.semaphore_signal(barrier, inc=1, device_id=(rep, lax.rem(me + k, 4)), device_id_type=MESH)
        load_x = pltpu.make_async_copy(x_hbm, x, in_sem.at[0])
        load_dy = pltpu.make_async_copy(dy_hbm, dy, in_sem.at[1])
        load_x.start()
        load_dy.start()
        load_x.wait()
        squares[...] = jnp.zeros_like(squares)

        def start(r):
            a[r, :] = normed(x[r, :])
            acc[r, :] = jnp.zeros((ROWS, D), F32)

        rows_loop(start)
        load_dy.wait()
        pl.semaphore_wait(barrier, 3)

    @pl.when(s < NT)
    def _():
        def forward(r):
            gate = dot(a[r, :], wg[...], 1, 0)
            up = dot(a[r, :], wu[...], 1, 0)
            hidden = (gate * jax.nn.sigmoid(gate) * up).astype(BF16)
            acc[r, :] += dot(hidden, wd[...], 1, 0)

        rows_loop(forward)

    @pl.when(s == NT)
    def _():
        def between(r):
            h[r, :] = x[r, :] + acc[r, :].astype(BF16)
            a[r, :] = normed(h[r, :])
            acc[r, :] = jnp.zeros((ROWS, D), F32)

        rows_loop(between)

    @pl.when(s == 2 * NT)
    def _():
        def between(r):
            da = acc[r, :].astype(BF16).astype(F32)
            wide = h[r, :].astype(F32)
            scale = lax.rsqrt(jnp.mean(wide * wide, -1, keepdims=True) + 1e-6)
            along = jnp.mean(da * wide, -1, keepdims=True)
            by_norm = da * scale - wide * (scale * scale * scale * along)
            dy[r, :] = dy[r, :] + by_norm.astype(BF16)
            a[r, :] = normed(x[r, :])

        rows_loop(between)

    @pl.when(s >= NT)
    def _():
        def hidden_grads(r):
            gate = dot(a[r, :], wg[...], 1, 0)
            up = dot(a[r, :], wu[...], 1, 0)
            dhid = dot(dy[r, :], wd[...], 1, 1).astype(BF16).astype(F32)
            sig = jax.nn.sigmoid(gate)
            silu = gate * sig
            hs[r, :] = (silu * up).astype(BF16)
            dus[r, :] = (dhid * silu).astype(BF16)
            dgs[r, :] = (dhid * up * (sig + silu * (1 - sig))).astype(BF16)

        half = TOKENS // 2
        rows_loop(hidden_grads, 0, half)

        @pl.when(t >= 1)
        def _():
            for c in to_partner(t - 1):
                c.wait()

        rows_loop(hidden_grads, half, TOKENS)
        chip_sum(t - 1)

        @pl.when(t >= 1)
        def _():
            for c in to_across(t - 1):
                c.start()

        @pl.when(t >= LAG)
        def _():
            for c in to_across(t - LAG):
                c.wait()

        @pl.when(s < 2 * NT)
        def _():
            def input_grads(r):
                by_both = jnp.concatenate([dgs[r, :], dus[r, :]], 1)
                acc[r, :] += dot(by_both, jnp.concatenate([wg[...], wu[...]], 1), 1, 1)

            rows_loop(input_grads)

        slot = lax.rem(t, 2)
        finish(t - LAG)
        mine_d[slot] = dot(hs[...], dy[...], 0, 0).astype(BF16)
        mine_gu[slot, 0] = dot(a[...], dgs[...], 0, 0).astype(BF16)
        mine_gu[slot, 1] = dot(a[...], dus[...], 0, 0).astype(BF16)
        for c in to_partner(t):
            c.start()

        @pl.when(t >= LAG)
        def _():
            put_out(t - LAG)

    @pl.when(s == NT + TILES - 1)
    def _():
        for c in to_partner(TILES - 1):
            c.wait()
        chip_sum(TILES - 1)
        for c in to_across(TILES - 1):
            c.start()

        def rest(i, carry):
            for c in to_across(i):
                c.wait()
            finish(i)
            put_out(i)
            return carry

        lax.fori_loop(TILES - LAG, TILES, rest, 0)
        ss_all[me] = squares[...]
        copies = [
            pltpu.make_async_remote_copy(
                squares, ss_all.at[me], s_send.at[k - 1], s_recv.at[me],
                device_id=(rep, lax.rem(me + k, 4)), device_id_type=MESH,
            )
            for k in range(1, 4)
        ]
        for c in copies:
            c.start()
        for c in copies:
            c.wait_send()
        for k in range(1, 4):
            who = lax.rem(me + k, 4)
            pltpu.make_async_remote_copy(
                squares, ss_all.at[who], s_send.at[k - 1], s_recv.at[who], device_id=(rep, who), device_id_type=MESH
            ).wait_recv()
        total = jnp.sum((ss_all[0] + ss_all[1]) + (ss_all[2] + ss_all[3]))
        factor[...] = jnp.minimum(1.0, 0.5 * lax.rsqrt(jnp.full((8, 128), total / COUNT + 1e-30, F32)))
        for piece, (first, last) in enumerate(PIECES):
            lax.fori_loop(first, last, lambda i, c: ([o.wait() for o in outs(i, piece)], c)[1], 0)


def gradients(x, dy, w_gate, w_up, w_down):
    any_space = pl.BlockSpec(memory_space=pl.ANY)
    layer = lambda s: lax.rem(lax.div(s, NT), 2)
    across = pl.BlockSpec((None, D, T), lambda s: (layer(s), 0, lax.rem(s, NT)))
    down = pl.BlockSpec((None, T, D), lambda s: (layer(s), lax.rem(s, NT), 0))
    sizes = [TILES, TILES] + [last - first for first, last in PIECES]
    shapes = [jax.ShapeDtypeStruct((3, QUARTER, size * T), BF16) for size in sizes]
    V, DMA = pltpu.VMEM, pltpu.SemaphoreType.DMA
    *results, factor = pl.pallas_call(
        grads_kernel,
        grid=(NT + TILES,),
        out_shape=(*shapes, jax.ShapeDtypeStruct((8, 128), F32)),
        in_specs=[any_space, any_space, across, across, down],
        out_specs=[any_space] * len(shapes) + [pl.BlockSpec((8, 128), lambda s: (0, 0))],
        scratch_shapes=[
            V((TOKENS, D), BF16), V((TOKENS, D), BF16), V((TOKENS, D), BF16), V((TOKENS, D), BF16), V((TOKENS, D), F32),
            V((TOKENS, T), BF16), V((TOKENS, T), BF16), V((TOKENS, T), BF16),
            V((2, 2, D, T), BF16), V((2, T, D), BF16),
            V((2, 2, HALF, T), BF16), V((2, T // 2, D), BF16),
            V((LAG + 1, 3, QUARTER, T), BF16), V((LAG + 1, 3, QUARTER, T), F32), V((TILES + LAG, 3, QUARTER, T), BF16),
            V((8, 128), F32), V((4, 8, 128), F32),
            DMA((2,)), DMA((2, 2)), DMA((2, 2)), DMA((LAG + 1,)), DMA((TILES,)), DMA((TILES, 2)),
            DMA((TILES,)), DMA((TILES,)), DMA((EARLY,)), DMA((EARLY,)), DMA((3,)), DMA((4,)),
        ],
        compiler_params=pltpu.CompilerParams(
            collective_id=0, has_side_effects=True, vmem_limit_bytes=67_000_000, dimension_semantics=("arbitrary",)
        ),
        cost_estimate=pl.CostEstimate(flops=17 * 2 * TOKENS * D * FF, bytes_accessed=100_000_000, transcendentals=0),
        name="grads",
    )(x, dy, w_gate, w_up, w_down)
    own, sibling, early, *pieces = results
    return own, sibling, early, pieces, factor


def adamw_kernel(tiles, steps, pos, factor, *refs):
    *qs, refs = (*refs[: len(steps)], refs[len(steps) :])
    scale, j = factor[0, 0], pl.program_id(0)

    def update(which, at_q, *at):
        (w, m, v), (new_w, new_m, new_v) = refs[which:9:3], refs[-9:][which::3]
        g = qs[0][at_q] if len(qs) == 1 else jnp.where(j < steps[0], qs[0][at_q], qs[1][at_q])
        g = g.astype(F32) * scale
        m1 = 0.9 * m[at] + 0.1 * g
        v1 = 0.95 * v[at] + 0.05 * g * g
        w0 = w[at].astype(F32)
        new_m[at] = m1
        new_v[at] = v1
        new_w[at] = (w0 - 0.02 * (m1 * lax.rsqrt(v1 + 1e-8) + 0.1 * w0)).astype(BF16)

    for which in range(2):
        update(which, which, slice(None), slice(None))
    for i in range(tiles):
        for there, (rows, cols) in FOLD:
            update(2, (2, rows, slice(cols.start + i * T, cols.stop + i * T)), i, *there)


def adamw(tiles, parts, pos, factor, weights, m, v, so_far):
    steps = [(last - first) // tiles for first, last, _, _ in parts]

    def at(j):
        (first, _, whose, _), (first1, _, whose1, _) = parts[0], parts[-1]
        later = j >= steps[0]
        first = jnp.where(later, first1 - tiles * steps[0], first) + tiles * j
        return 1 - first // NT, first % NT // tiles, jnp.where(later, whose1, whose)

    def across_at(j, pos):
        layer, block, whose = at(j)
        return layer, pos[whose], block

    def down_at(j, pos):
        layer, block, whose = at(j)
        return layer, block, pos[whose], 0, 0

    across = pl.BlockSpec((None, QUARTER, tiles * T), across_at)
    down = pl.BlockSpec((None, tiles, None, T // 4, D), down_at)
    three = [across, across, down]
    q_at = [lambda j, pos: (0, 0, jnp.minimum(j, steps[0] - 1)), lambda j, pos: (0, 0, jnp.maximum(j - steps[0], 0))]
    return pl.pallas_call(
        functools.partial(adamw_kernel, tiles, steps),
        grid_spec=pltpu.PrefetchScalarGridSpec(
            num_scalar_prefetch=1,
            grid=(sum(steps),),
            in_specs=[pl.BlockSpec(memory_space=pltpu.SMEM)]
            + [pl.BlockSpec((3, QUARTER, tiles * T), q_at[i]) for i in range(len(parts))]
            + three * 3
            + [pl.BlockSpec(memory_space=pl.ANY)] * len(so_far),
            out_specs=three * 3,
        ),
        out_shape=tuple(jax.ShapeDtypeStruct(w.shape, d) for d in (BF16, F32, F32) for w in weights),
        input_output_aliases={11 + len(parts) + i: i for i in range(len(so_far))},
        compiler_params=pltpu.CompilerParams(vmem_limit_bytes=64_000_000),
        cost_estimate=pl.CostEstimate(flops=0, bytes_accessed=17 * D * T * tiles * sum(steps), transcendentals=0),
        name="adamw",
    )(pos, factor, *[part[3] for part in parts], *weights, *m, *v, *so_far)


def solution(mesh):
    swap_cores = [(0, 1), (1, 0), (2, 3), (3, 2)]
    swap_chips = [(0, 2), (2, 0), (1, 3), (3, 1)]

    def whole(x, dy, *arrays):
        weights, m, v = (arrays[i : i + 3] for i in (0, 3, 6))
        own, sibling, early, pieces, factor = gradients(x[0], dy[0], *weights)
        me = lax.axis_index("dp")
        core, chip = me % 2, me // 2
        pos = jnp.stack([core * 2 + chip, (1 - core) * 2 + chip, core * 2 + 1 - chip, (1 - core) * 2 + 1 - chip]).astype(jnp.int32)
        weights, m, v = ([*three[:2], three[2].reshape(LAYERS, NT, 4, T // 4, D)] for three in (weights, m, v))
        others = [early]
        for n in range(1, N):
            others.append(lax.ppermute(pieces[n - 1], "dp", swap_chips))
        inner = lax.ppermute(early, "dp", swap_cores)
        new = adamw(5, [(0, TILES, 0, own), (0, TILES, 1, sibling)], pos, factor, weights, m, v, ())
        first, last = PIECES[0]
        new = adamw(2, [(first, last, 2, early), (first, last, 3, inner)], pos, factor, weights, m, v, new)
        for n, (first, last) in enumerate(PIECES[1:], 1):
            other, new = lax.optimization_barrier((others[n], new))
            inner = lax.ppermute(other, "dp", swap_cores)
            new = adamw(2, [(first, last, 2, other)], pos, factor, weights, m, v, new)
            new = adamw(2, [(first, last, 3, inner)], pos, factor, weights, m, v, new)
        return tuple(one.reshape(LAYERS, FF, D) if one.ndim == 5 else one for one in new)

    return jax.shard_map(
        whole,
        mesh=mesh,
        in_specs=(P(("rep", "dp"), None, None),) * 2 + (P(None, None, None),) * 9,
        out_specs=(P("rep", None, None),) * 9,
        check_vma=False,
    )
```

profile of v0, /device:TPU:0, one launch (start us, length us, event | category | flops | bytes accessed | tf_op | source)
XLA Modules:
  0.0 409.4 jit_solution(16663103276523881360)
XLA Ops:
  0.6 249.0 %grads.1 = (bf16[3,224,5120]{2,1,0:T(8,128)(2,1)}, bf16[3,224,5120]{2,1,0:T(8,128)(2,1)}, bf16[3,224,1024]{2,1,0:T(8,128)(2,1)}, bf16[3,224,1536]{2,1,0:T(8,128)...) custom-call(bf16[2048,896]{1,0:T(8,128)(2,1)} %bitcast.45, ...), custom_call_target="tpu_custom_call" | custom-call | flops 159719096320 | bytes 100000000 | tf_op jit(solution)/shard_map/grads/pallas_call | solution.py:281
  249.7 2.2 collective-permute-start.3
  251.9 0.7 pad_add_fusion.pos
  252.6 49.3 %adamw.10 = (bf16[2,896,2560]{2,1,0:T(8,128)(2,1)}, bf16[2,896,2560]{2,1,0:T(8,128)(2,1)}, bf16[2,10,4,64,896]{4,3,2,1,0:T(8,128)(2,1)}, f32[2,896,2560]{2,1,0:T...) custom-call(s32[4]{0:T(128)} %pad_add_fusion.pos, ...), custom_call_target="tpu_custom_call" | custom-call | bytes 155975680 | tf_op jit(solution)/shard_map/adamw/pallas_call | solution.py:350
  301.9 12.2 %adamw.11 = (bf16[2,896,2560]{2,1,0:T(8,128)(2,1)}, bf16[2,896,2560]{2,1,0:T(8,128)(2,1)}, bf16[2,10,4,64,896]{4,3,2,1,0:T(8,128)(2,1)}, f32[2,896,2560]{2,1,0:T...) custom-call(s32[4]{0:T(128)} %pad_add_fusion.pos, ...), custom_call_target="tpu_custom_call", output_to_operand_aliasing={{0}: (13, {}), {1}: (14, {}), {2}: (15, {}), {3}: (16, {}),... | custom-call | bytes 31195136 | tf_op jit(solution)/shard_map/adamw/pallas_call | solution.py:350
  314.1 0.5 collective-permute-start.5
  314.5 0.0 collective-permute-start.2
  314.6 0.8 copy-done
  315.4 11.0 %adamw.12 = (bf16[2,896,2560]{2,1,0:T(8,128)(2,1)}, bf16[2,896,2560]{2,1,0:T(8,128)(2,1)}, bf16[2,10,4,64,896]{4,3,2,1,0:T(8,128)(2,1)}, f32[2,896,2560]{2,1,0:T...) custom-call(s32[4]{0:T(128)} %pad_add_fusion.pos, ...), custom_call_target="tpu_custom_call", output_to_operand_aliasing={{0}: (12, {}), {1}: (13, {}), {2}: (14, {}), {3}: (15, {}),... | custom-call | bytes 23396352 | tf_op jit(solution)/shard_map/adamw/pallas_call | solution.py:350
  326.4 11.1 %adamw.13 = (bf16[2,896,2560]{2,1,0:T(8,128)(2,1)}, bf16[2,896,2560]{2,1,0:T(8,128)(2,1)}, bf16[2,10,4,64,896]{4,3,2,1,0:T(8,128)(2,1)}, f32[2,896,2560]{2,1,0:T...) custom-call(s32[4]{0:T(128)} %pad_add_fusion.pos, ...), custom_call_target="tpu_custom_call", output_to_operand_aliasing={{0}: (12, {}), {1}: (13, {}), {2}: (14, {}), {3}: (15, {}),... | custom-call | bytes 23396352 | tf_op jit(solution)/shard_map/adamw/pallas_call | solution.py:350
  337.4 9.6 %collective-permute-done.2.refs_0_ = bf16[3,224,1024]{2,1,0:T(8,128)(2,1)} collective-permute-done((bf16[3,224,1024]{2,1,0:T(8,128)(2,1)}, bf16[3,224,1024]{2,1,0:T(8,128)(2,1)}, u32[]{:S(2)}, u32[]{:S(2)}) %collective-permute-start.2) | collective-permute-done | bytes 1376288 | tf_op jit(solution)/shard_map/ppermute | solution.py:382
  347.0 0.3 collective-permute-start.1
  347.3 6.8 %adamw.14 = (bf16[2,896,2560]{2,1,0:T(8,128)(2,1)}, bf16[2,896,2560]{2,1,0:T(8,128)(2,1)}, bf16[2,10,4,64,896]{4,3,2,1,0:T(8,128)(2,1)}, f32[2,896,2560]{2,1,0:T...) custom-call(s32[4]{0:T(128)} %pad_add_fusion.pos, ...), custom_call_target="tpu_custom_call", output_to_operand_aliasing={{0}: (12, {}), {1}: (13, {}), {2}: (14, {}), {3}: (15, {}),... | custom-call | bytes 15597568 | tf_op jit(solution)/shard_map/adamw/pallas_call | solution.py:350
  354.1 1.1 copy-done.2
  355.2 6.8 %adamw.15 = (bf16[2,896,2560]{2,1,0:T(8,128)(2,1)}, bf16[2,896,2560]{2,1,0:T(8,128)(2,1)}, bf16[2,10,4,64,896]{4,3,2,1,0:T(8,128)(2,1)}, f32[2,896,2560]{2,1,0:T...) custom-call(s32[4]{0:T(128)} %pad_add_fusion.pos, ...), custom_call_target="tpu_custom_call", output_to_operand_aliasing={{0}: (12, {}), {1}: (13, {}), {2}: (14, {}), {3}: (15, {}),... | custom-call | bytes 15597568 | tf_op jit(solution)/shard_map/adamw/pallas_call | solution.py:350
  362.1 17.9 %collective-permute-done.1.refs_0_ = bf16[3,224,1024]{2,1,0:T(8,128)(2,1)} collective-permute-done((bf16[3,224,1024]{2,1,0:T(8,128)(2,1)}, bf16[3,224,1024]{2,1,0:T(8,128)(2,1)}, u32[]{:S(2)}, u32[]{:S(2)}) %collective-permute-start.1) | collective-permute-done | bytes 1376288 | tf_op jit(solution)/shard_map/ppermute | solution.py:382
  379.9 0.3 collective-permute-start
  380.2 6.9 %adamw.16 = (bf16[2,896,2560]{2,1,0:T(8,128)(2,1)}, bf16[2,896,2560]{2,1,0:T(8,128)(2,1)}, bf16[2,10,4,64,896]{4,3,2,1,0:T(8,128)(2,1)}, f32[2,896,2560]{2,1,0:T...) custom-call(s32[4]{0:T(128)} %pad_add_fusion.pos, ...), custom_call_target="tpu_custom_call", output_to_operand_aliasing={{0}: (12, {}), {1}: (13, {}), {2}: (14, {}), {3}: (15, {}),... | custom-call | bytes 15597568 | tf_op jit(solution)/shard_map/adamw/pallas_call | solution.py:350
  387.1 1.1 copy-done.1
  388.2 7.1 %adamw.17 = (bf16[2,896,2560]{2,1,0:T(8,128)(2,1)}, bf16[2,896,2560]{2,1,0:T(8,128)(2,1)}, bf16[2,10,4,64,896]{4,3,2,1,0:T(8,128)(2,1)}, f32[2,896,2560]{2,1,0:T...) custom-call(s32[4]{0:T(128)} %pad_add_fusion.pos, ...), custom_call_target="tpu_custom_call", output_to_operand_aliasing={{0}: (12, {}), {1}: (13, {}), {2}: (14, {}), {3}: (15, {}),... | custom-call | bytes 15597568 | tf_op jit(solution)/shard_map/adamw/pallas_call | solution.py:350
  395.2 2.8 collective-permute-done.refs_0_
  398.1 5.2 %adamw.18 = (bf16[2,896,2560]{2,1,0:T(8,128)(2,1)}, bf16[2,896,2560]{2,1,0:T(8,128)(2,1)}, bf16[2,10,4,64,896]{4,3,2,1,0:T(8,128)(2,1)}, f32[2,896,2560]{2,1,0:T...) custom-call(s32[4]{0:T(128)} %pad_add_fusion.pos, ...), custom_call_target="tpu_custom_call", output_to_operand_aliasing={{0}: (12, {}), {1}: (13, {}), {2}: (14, {}), {3}: (15, {}),... | custom-call | bytes 7798784 | tf_op jit(solution)/shard_map/adamw/pallas_call | solution.py:350
  403.3 0.9 copy-done.3
  404.2 5.2 %adamw.19 = (bf16[2,896,2560]{2,1,0:T(8,128)(2,1)}, bf16[2,896,2560]{2,1,0:T(8,128)(2,1)}, bf16[2,10,4,64,896]{4,3,2,1,0:T(8,128)(2,1)}, f32[2,896,2560]{2,1,0:T...) custom-call(s32[4]{0:T(128)} %pad_add_fusion.pos, ...), custom_call_target="tpu_custom_call", output_to_operand_aliasing={{0}: (12, {}), {1}: (13, {}), {2}: (14, {}), {3}: (15, {}),... | custom-call | bytes 7798784 | tf_op jit(solution)/shard_map/adamw/pallas_call | solution.py:350
  (14 shorter events, 0.0 us)
Async XLA Ops:
  249.7 64.4 %collective-permute-start.3 = (bf16[3,224,1536]{2,1,0:T(8,128)(2,1)}, bf16[3,224,1536]{2,1,0:T(8,128)(2,1)S(1)}, u32[]{:S(2)}, u32[]{:S(2)}) collective-permute-start(bf16[3,224,1536]{2,1,0:T(8,128)(2,1)} %get-tuple-element.151), channel_id=1, source_target_pairs={{0,2},{2,0},{1,3},{3,1},{4,6},{6,4},{5,7},{7,5}} | collective-permute-start | bytes 6193160 | tf_op jit(solution)/shard_map/ppermute | solution.py:382
  251.9 50.0 %collective-permute-start.4 = (bf16[3,224,1024]{2,1,0:T(8,128)(2,1)}, bf16[3,224,1024]{2,1,0:T(8,128)(2,1)}, u32[]{:S(2)}, u32[]{:S(2)}) collective-permute-start(bf16[3,224,1024]{2,1,0:T(8,128)(2,1)} %get-tuple-element.152.refs_0_), channel_id=1, source_target_pairs={{0,1},{1,0},{2,3},{3,2},{4,5},{5,4},{6,7},{7,6}} | collective-permute-start | bytes 4128776 | tf_op jit(solution)/shard_map/ppermute | solution.py:383
  314.1 1.3 copy-start
  314.1 12.3 %collective-permute-start.5 = (bf16[3,224,1536]{2,1,0:T(8,128)(2,1)S(1)}, bf16[3,224,1536]{2,1,0:T(8,128)(2,1)}, u32[]{:S(2)}, u32[]{:S(2)}) collective-permute-start(bf16[3,224,1536]{2,1,0:T(8,128)(2,1)S(1)} %collective-permute-done.3.refs_0_), channel_id=1, source_target_pairs={{0,1},{1,0},{2,3},{3,2},{4,5},{5,4},{6,7},{7,6}} | collective-permute-start | bytes 6193160 | tf_op jit(solution)/shard_map/ppermute | solution.py:389
  314.5 32.5 %collective-permute-start.2 = (bf16[3,224,1024]{2,1,0:T(8,128)(2,1)}, bf16[3,224,1024]{2,1,0:T(8,128)(2,1)}, u32[]{:S(2)}, u32[]{:S(2)}) collective-permute-start(bf16[3,224,1024]{2,1,0:T(8,128)(2,1)} %get-tuple-element.150), channel_id=1, source_target_pairs={{0,2},{2,0},{1,3},{3,1},{4,6},{6,4},{5,7},{7,5}} | collective-permute-start | bytes 4128776 | tf_op jit(solution)/shard_map/ppermute | solution.py:382
  347.0 7.1 %collective-permute-start.6 = (bf16[3,224,1024]{2,1,0:T(8,128)(2,1)}, bf16[3,224,1024]{2,1,0:T(8,128)(2,1)S(1)}, u32[]{:S(2)}, u32[]{:S(2)}) collective-permute-start(bf16[3,224,1024]{2,1,0:T(8,128)(2,1)} %collective-permute-done.2.refs_0_), channel_id=1, source_target_pairs={{0,1},{1,0},{2,3},{3,2},{4,5},{5,4},{6,7},{7,6}} | collective-permute-start | bytes 4128776 | tf_op jit(solution)/shard_map/ppermute | solution.py:389
  347.0 32.9 %collective-permute-start.1 = (bf16[3,224,1024]{2,1,0:T(8,128)(2,1)}, bf16[3,224,1024]{2,1,0:T(8,128)(2,1)}, u32[]{:S(2)}, u32[]{:S(2)}) collective-permute-start(bf16[3,224,1024]{2,1,0:T(8,128)(2,1)} %get-tuple-element.149), channel_id=1, source_target_pairs={{0,2},{2,0},{1,3},{3,1},{4,6},{6,4},{5,7},{7,5}} | collective-permute-start | bytes 4128776 | tf_op jit(solution)/shard_map/ppermute | solution.py:382
  354.1 1.1 copy-start.2
  379.9 7.2 %collective-permute-start.7 = (bf16[3,224,1024]{2,1,0:T(8,128)(2,1)}, bf16[3,224,1024]{2,1,0:T(8,128)(2,1)S(1)}, u32[]{:S(2)}, u32[]{:S(2)}) collective-permute-start(bf16[3,224,1024]{2,1,0:T(8,128)(2,1)} %collective-permute-done.1.refs_0_), channel_id=1, source_target_pairs={{0,1},{1,0},{2,3},{3,2},{4,5},{5,4},{6,7},{7,6}} | collective-permute-start | bytes 4128776 | tf_op jit(solution)/shard_map/ppermute | solution.py:389
  379.9 18.2 %collective-permute-start = (bf16[3,224,512]{2,1,0:T(8,128)(2,1)}, bf16[3,224,512]{2,1,0:T(8,128)(2,1)}, u32[]{:S(2)}, u32[]{:S(2)}) collective-permute-start(bf16[3,224,512]{2,1,0:T(8,128)(2,1)} %get-tuple-element.148), channel_id=1, source_target_pairs={{0,2},{2,0},{1,3},{3,1},{4,6},{6,4},{5,7},{7,5}} | collective-permute-start | bytes 2064392 | tf_op jit(solution)/shard_map/ppermute | solution.py:382
  387.1 1.1 copy-start.1
  398.1 5.2 %collective-permute-start.8 = (bf16[3,224,512]{2,1,0:T(8,128)(2,1)}, bf16[3,224,512]{2,1,0:T(8,128)(2,1)S(1)}, u32[]{:S(2)}, u32[]{:S(2)}) collective-permute-start(bf16[3,224,512]{2,1,0:T(8,128)(2,1)} %collective-permute-done.refs_0_), channel_id=1, source_target_pairs={{0,1},{1,0},{2,3},{3,2},{4,5},{5,4},{6,7},{7,6}} | collective-permute-start | bytes 2064392 | tf_op jit(solution)/shard_map/ppermute | solution.py:389
  403.3 0.9 copy-start.3
where the time goes:
time: 410 us; the launch traced here: 409 us
  Pallas kernels  371 us (90%)
  waiting for transfers between devices  30.3 us (7%)
    pallas_call x1, Pallas kernels, gradients(): pl.pallas_call(grads_kernel, grid=(NT + TILES,), out_shape=(*shapes, jax....  249 us
    pallas_call x10, Pallas kernels, adamw(): pl.pallas_call(functools.partial(adamw_kernel, tiles, steps), grid_spec=p...  122 us
    ppermute x4, waiting for transfers between devices, whole(): others.append(lax.ppermute(pieces[n - 1], 'dp', swap_chips))  30.3 us
  transfers between devices with their start and end apart: 9, of which 3 were waited for; matrix products, arithmetic and copies ran while one was open for 0% of the time, Pallas kernels for 28%

commit v1 on v0

--- a/solution.py
+++ b/solution.py
@@ -16,8 +16,8 @@
 TILES = LAYERS * NT
 ROWS = 512
 HALF, QUARTER = D // 2, D // 4
-LAG = 5
-PIECES = ((0, 4), (4, 10), (10, 14), (14, 18), (18, 20))
+LAG = 4
+PIECES = ((0, 2), (2, 8), (8, 14), (14, 17), (17, 19), (19, 20))
 N = len(PIECES)
 EARLY = PIECES[0][1]
 COUNT = 3 * LAYERS * D * FF
@@ -383,12 +383,13 @@
         inner = lax.ppermute(early, "dp", swap_cores)
         new = adamw(5, [(0, TILES, 0, own), (0, TILES, 1, sibling)], pos, factor, weights, m, v, ())
         first, last = PIECES[0]
-        new = adamw(2, [(first, last, 2, early), (first, last, 3, inner)], pos, factor, weights, m, v, new)
+        new = adamw(1, [(first, last, 2, early), (first, last, 3, inner)], pos, factor, weights, m, v, new)
         for n, (first, last) in enumerate(PIECES[1:], 1):
             other, new = lax.optimization_barrier((others[n], new))
             inner = lax.ppermute(other, "dp", swap_cores)
-            new = adamw(2, [(first, last, 2, other)], pos, factor, weights, m, v, new)
-            new = adamw(2, [(first, last, 3, inner)], pos, factor, weights, m, v, new)
+            tiles = 1 if last - first < 4 else 2
+            new = adamw(tiles, [(first, last, 2, other)], pos, factor, weights, m, v, new)
+            new = adamw(tiles, [(first, last, 3, inner)], pos, factor, weights, m, v, new)
         return tuple(one.reshape(LAYERS, FF, D) if one.ndim == 5 else one for one in new)
 
     return jax.shard_map(

time: 410 us -> 407 us (level)
  Pallas kernels: 371 us -> 366 us
    pallas_call x1, Pallas kernels: 249 us -> 234 us  [gradients(): pl.pallas_call(grads_kernel, grid=(NT + TILES,), out_shape=(*shapes, jax....]
    pallas_call x10 -> x12, Pallas kernels: 122 us -> 132 us  [adamw(): pl.pallas_call(functools.partial(adamw_kernel, tiles, steps), grid_spec=p...]
    ppermute x4 -> x5, waiting for transfers between devices: 30.3 us -> 29 us  [whole(): others.append(lax.ppermute(pieces[n - 1], 'dp', swap_chips))]
  transfers between devices with their start and end apart: 9 -> 11, of which waited for: 3 -> 4; matrix products, arithmetic and copies ran while one was open for 0% -> 0% of each run, Pallas kernels for 28% -> 32%
where the time goes in v1:
time: 407 us; the launch traced here: 406 us
  Pallas kernels  366 us (90%)
  waiting for transfers between devices  29 us (7%)
  local copies, waits for them, and re-layouts  5.62 us (1%)
    pallas_call x1, Pallas kernels, gradients(): pl.pallas_call(grads_kernel, grid=(NT + TILES,), out_shape=(*shapes, jax....  234 us
    pallas_call x12, Pallas kernels, adamw(): pl.pallas_call(functools.partial(adamw_kernel, tiles, steps), grid_spec=p...  132 us
    ppermute x5, waiting for transfers between devices, whole(): others.append(lax.ppermute(pieces[n - 1], 'dp', swap_chips))  29 us
  transfers between devices with their start and end apart: 11, of which 4 were waited for; matrix products, arithmetic and copies ran while one was open for 0% of the time, Pallas kernels for 32%

profile of v1, /device:TPU:0, one launch (start us, length us, event | category | flops | bytes accessed | tf_op | source)
XLA Modules:
  0.0 406.2 jit_solution(12644658611434588649)
XLA Ops:
  0.6 234.3 %grads.1 = (bf16[3,224,5120]{2,1,0:T(8,128)(2,1)}, bf16[3,224,5120]{2,1,0:T(8,128)(2,1)}, bf16[3,224,512]{2,1,0:T(8,128)(2,1)}, bf16[3,224,1536]{2,1,0:T(8,128)(...) custom-call(bf16[2048,896]{1,0:T(8,128)(2,1)} %bitcast.51, ...), custom_call_target="tpu_custom_call" | custom-call | flops 159719096320 | bytes 100000000 | tf_op jit(solution)/shard_map/grads/pallas_call | solution.py:281
  235.0 2.2 collective-permute-start.4
  237.2 0.6 pad_add_fusion.pos
  237.8 49.4 %adamw.12 = (bf16[2,896,2560]{2,1,0:T(8,128)(2,1)}, bf16[2,896,2560]{2,1,0:T(8,128)(2,1)}, bf16[2,10,4,64,896]{4,3,2,1,0:T(8,128)(2,1)}, f32[2,896,2560]{2,1,0:T...) custom-call(s32[4]{0:T(128)} %pad_add_fusion.pos, ...), custom_call_target="tpu_custom_call" | custom-call | bytes 155975680 | tf_op jit(solution)/shard_map/adamw/pallas_call | solution.py:350
  287.2 0.8 copy-done.3
  288.0 7.9 %adamw.13 = (bf16[2,896,2560]{2,1,0:T(8,128)(2,1)}, bf16[2,896,2560]{2,1,0:T(8,128)(2,1)}, bf16[2,10,4,64,896]{4,3,2,1,0:T(8,128)(2,1)}, f32[2,896,2560]{2,1,0:T...) custom-call(s32[4]{0:T(128)} %pad_add_fusion.pos, ...), custom_call_target="tpu_custom_call", output_to_operand_aliasing={{0}: (13, {}), {1}: (14, {}), {2}: (15, {}), {3}: (16, {}),... | custom-call | bytes 15597568 | tf_op jit(solution)/shard_map/adamw/pallas_call | solution.py:350
  296.3 0.9 copy-done
  297.2 11.0 %adamw.14 = (bf16[2,896,2560]{2,1,0:T(8,128)(2,1)}, bf16[2,896,2560]{2,1,0:T(8,128)(2,1)}, bf16[2,10,4,64,896]{4,3,2,1,0:T(8,128)(2,1)}, f32[2,896,2560]{2,1,0:T...) custom-call(s32[4]{0:T(128)} %pad_add_fusion.pos, ...), custom_call_target="tpu_custom_call", output_to_operand_aliasing={{0}: (12, {}), {1}: (13, {}), {2}: (14, {}), {3}: (15, {}),... | custom-call | bytes 23396352 | tf_op jit(solution)/shard_map/adamw/pallas_call | solution.py:350
  308.2 11.1 %adamw.15 = (bf16[2,896,2560]{2,1,0:T(8,128)(2,1)}, bf16[2,896,2560]{2,1,0:T(8,128)(2,1)}, bf16[2,10,4,64,896]{4,3,2,1,0:T(8,128)(2,1)}, f32[2,896,2560]{2,1,0:T...) custom-call(s32[4]{0:T(128)} %pad_add_fusion.pos, ...), custom_call_target="tpu_custom_call", output_to_operand_aliasing={{0}: (12, {}), {1}: (13, {}), {2}: (14, {}), {3}: (15, {}),... | custom-call | bytes 23396352 | tf_op jit(solution)/shard_map/adamw/pallas_call | solution.py:350
  319.3 24.3 %collective-permute-done.3.refs_0_ = bf16[3,224,1536]{2,1,0:T(8,128)(2,1)} collective-permute-done((bf16[3,224,1536]{2,1,0:T(8,128)(2,1)}, bf16[3,224,1536]{2,1,0:T(8,128)(2,1)}, u32[]{:S(2)}, u32[]{:S(2)}) %collective-permute-start.3) | collective-permute-done | bytes 2064416 | tf_op jit(solution)/shard_map/ppermute | solution.py:382
  343.8 11.0 %adamw.16 = (bf16[2,896,2560]{2,1,0:T(8,128)(2,1)}, bf16[2,896,2560]{2,1,0:T(8,128)(2,1)}, bf16[2,10,4,64,896]{4,3,2,1,0:T(8,128)(2,1)}, f32[2,896,2560]{2,1,0:T...) custom-call(s32[4]{0:T(128)} %pad_add_fusion.pos, ...), custom_call_target="tpu_custom_call", output_to_operand_aliasing={{0}: (12, {}), {1}: (13, {}), {2}: (14, {}), {3}: (15, {}),... | custom-call | bytes 23396352 | tf_op jit(solution)/shard_map/adamw/pallas_call | solution.py:350
  354.9 1.3 copy-done.1
  356.2 11.0 %adamw.17 = (bf16[2,896,2560]{2,1,0:T(8,128)(2,1)}, bf16[2,896,2560]{2,1,0:T(8,128)(2,1)}, bf16[2,10,4,64,896]{4,3,2,1,0:T(8,128)(2,1)}, f32[2,896,2560]{2,1,0:T...) custom-call(s32[4]{0:T(128)} %pad_add_fusion.pos, ...), custom_call_target="tpu_custom_call", output_to_operand_aliasing={{0}: (12, {}), {1}: (13, {}), {2}: (14, {}), {3}: (15, {}),... | custom-call | bytes 23396352 | tf_op jit(solution)/shard_map/adamw/pallas_call | solution.py:350
  367.2 1.9 collective-permute-done.2.refs_0_
  369.4 7.1 %adamw.18 = (bf16[2,896,2560]{2,1,0:T(8,128)(2,1)}, bf16[2,896,2560]{2,1,0:T(8,128)(2,1)}, bf16[2,10,4,64,896]{4,3,2,1,0:T(8,128)(2,1)}, f32[2,896,2560]{2,1,0:T...) custom-call(s32[4]{0:T(128)} %pad_add_fusion.pos, ...), custom_call_target="tpu_custom_call", output_to_operand_aliasing={{0}: (12, {}), {1}: (13, {}), {2}: (14, {}), {3}: (15, {}),... | custom-call | bytes 11698176 | tf_op jit(solution)/shard_map/adamw/pallas_call | solution.py:350
  376.5 1.0 copy-done.2
  377.5 7.1 %adamw.19 = (bf16[2,896,2560]{2,1,0:T(8,128)(2,1)}, bf16[2,896,2560]{2,1,0:T(8,128)(2,1)}, bf16[2,10,4,64,896]{4,3,2,1,0:T(8,128)(2,1)}, f32[2,896,2560]{2,1,0:T...) custom-call(s32[4]{0:T(128)} %pad_add_fusion.pos, ...), custom_call_target="tpu_custom_call", output_to_operand_aliasing={{0}: (12, {}), {1}: (13, {}), {2}: (14, {}), {3}: (15, {}),... | custom-call | bytes 11698176 | tf_op jit(solution)/shard_map/adamw/pallas_call | solution.py:350
  384.6 2.7 collective-permute-done.1.refs_0_
  387.5 4.9 %adamw.20 = (bf16[2,896,2560]{2,1,0:T(8,128)(2,1)}, bf16[2,896,2560]{2,1,0:T(8,128)(2,1)}, bf16[2,10,4,64,896]{4,3,2,1,0:T(8,128)(2,1)}, f32[2,896,2560]{2,1,0:T...) custom-call(s32[4]{0:T(128)} %pad_add_fusion.pos, ...), custom_call_target="tpu_custom_call", output_to_operand_aliasing={{0}: (12, {}), {1}: (13, {}), {2}: (14, {}), {3}: (15, {}),... | custom-call | bytes 7798784 | tf_op jit(solution)/shard_map/adamw/pallas_call | solution.py:350
  392.5 0.8 copy-done.4
  393.3 4.7 %adamw.21 = (bf16[2,896,2560]{2,1,0:T(8,128)(2,1)}, bf16[2,896,2560]{2,1,0:T(8,128)(2,1)}, bf16[2,10,4,64,896]{4,3,2,1,0:T(8,128)(2,1)}, f32[2,896,2560]{2,1,0:T...) custom-call(s32[4]{0:T(128)} %pad_add_fusion.pos, ...), custom_call_target="tpu_custom_call", output_to_operand_aliasing={{0}: (12, {}), {1}: (13, {}), {2}: (14, {}), {3}: (15, {}),... | custom-call | bytes 7798784 | tf_op jit(solution)/shard_map/adamw/pallas_call | solution.py:350
  398.2 3.5 adamw.22
  401.8 0.7 copy-done.5
  402.5 3.5 adamw.23
  (24 shorter events, 1.5 us)
Async XLA Ops:
  235.0 60.9 %collective-permute-start.4 = (bf16[3,224,1536]{2,1,0:T(8,128)(2,1)}, bf16[3,224,1536]{2,1,0:T(8,128)(2,1)S(1)}, u32[]{:S(2)}, u32[]{:S(2)}) collective-permute-start(bf16[3,224,1536]{2,1,0:T(8,128)(2,1)} %get-tuple-element.181), channel_id=1, source_target_pairs={{0,2},{2,0},{1,3},{3,1},{4,6},{6,4},{5,7},{7,5}} | collective-permute-start | bytes 6193160 | tf_op jit(solution)/shard_map/ppermute | solution.py:382
  237.2 49.9 %collective-permute-start.5 = (bf16[3,224,512]{2,1,0:T(8,128)(2,1)}, bf16[3,224,512]{2,1,0:T(8,128)(2,1)S(1)}, u32[]{:S(2)}, u32[]{:S(2)}) collective-permute-start(bf16[3,224,512]{2,1,0:T(8,128)(2,1)} %get-tuple-element.182.refs_0_), channel_id=1, source_target_pairs={{0,1},{1,0},{2,3},{3,2},{4,5},{5,4},{6,7},{7,6}} | collective-permute-start | bytes 2064392 | tf_op jit(solution)/shard_map/ppermute | solution.py:383
  287.1 0.8 copy-start.3
  295.9 1.3 copy-start
  295.9 12.3 %collective-permute-start.6 = (bf16[3,224,1536]{2,1,0:T(8,128)(2,1)S(1)}, bf16[3,224,1536]{2,1,0:T(8,128)(2,1)}, u32[]{:S(2)}, u32[]{:S(2)}) collective-permute-start(bf16[3,224,1536]{2,1,0:T(8,128)(2,1)S(1)} %collective-permute-done.4.refs_0_), channel_id=1, source_target_pairs={{0,1},{1,0},{2,3},{3,2},{4,5},{5,4},{6,7},{7,6}} | collective-permute-start | bytes 6193160 | tf_op jit(solution)/shard_map/ppermute | solution.py:389
  296.2 47.3 %collective-permute-start.3 = (bf16[3,224,1536]{2,1,0:T(8,128)(2,1)}, bf16[3,224,1536]{2,1,0:T(8,128)(2,1)}, u32[]{:S(2)}, u32[]{:S(2)}) collective-permute-start(bf16[3,224,1536]{2,1,0:T(8,128)(2,1)} %get-tuple-element.180), channel_id=1, source_target_pairs={{0,2},{2,0},{1,3},{3,1},{4,6},{6,4},{5,7},{7,5}} | collective-permute-start | bytes 6193160 | tf_op jit(solution)/shard_map/ppermute | solution.py:382
  343.6 11.3 %collective-permute-start.7 = (bf16[3,224,1536]{2,1,0:T(8,128)(2,1)}, bf16[3,224,1536]{2,1,0:T(8,128)(2,1)S(1)}, u32[]{:S(2)}, u32[]{:S(2)}) collective-permute-start(bf16[3,224,1536]{2,1,0:T(8,128)(2,1)} %collective-permute-done.3.refs_0_), channel_id=1, source_target_pairs={{0,1},{1,0},{2,3},{3,2},{4,5},{5,4},{6,7},{7,6}} | collective-permute-start | bytes 6193160 | tf_op jit(solution)/shard_map/ppermute | solution.py:389
  343.6 25.5 %collective-permute-start.2 = (bf16[3,224,768]{2,1,0:T(8,128)(2,1)}, bf16[3,224,768]{2,1,0:T(8,128)(2,1)}, u32[]{:S(2)}, u32[]{:S(2)}) collective-permute-start(bf16[3,224,768]{2,1,0:T(8,128)(2,1)} %get-tuple-element.179), channel_id=1, source_target_pairs={{0,2},{2,0},{1,3},{3,1},{4,6},{6,4},{5,7},{7,5}} | collective-permute-start | bytes 3096584 | tf_op jit(solution)/shard_map/ppermute | solution.py:382
  354.8 1.3 copy-start.1
  369.1 7.4 %collective-permute-start.8 = (bf16[3,224,768]{2,1,0:T(8,128)(2,1)}, bf16[3,224,768]{2,1,0:T(8,128)(2,1)S(1)}, u32[]{:S(2)}, u32[]{:S(2)}) collective-permute-start(bf16[3,224,768]{2,1,0:T(8,128)(2,1)} %collective-permute-done.2.refs_0_), channel_id=1, source_target_pairs={{0,1},{1,0},{2,3},{3,2},{4,5},{5,4},{6,7},{7,6}} | collective-permute-start | bytes 3096584 | tf_op jit(solution)/shard_map/ppermute | solution.py:389
  369.1 18.2 %collective-permute-start.1 = (bf16[3,224,512]{2,1,0:T(8,128)(2,1)}, bf16[3,224,512]{2,1,0:T(8,128)(2,1)}, u32[]{:S(2)}, u32[]{:S(2)}) collective-permute-start(bf16[3,224,512]{2,1,0:T(8,128)(2,1)} %get-tuple-element.178), channel_id=1, source_target_pairs={{0,2},{2,0},{1,3},{3,1},{4,6},{6,4},{5,7},{7,5}} | collective-permute-start | bytes 2064392 | tf_op jit(solution)/shard_map/ppermute | solution.py:382
  376.5 1.0 copy-start.2
  387.3 5.2 %collective-permute-start.9 = (bf16[3,224,512]{2,1,0:T(8,128)(2,1)}, bf16[3,224,512]{2,1,0:T(8,128)(2,1)S(1)}, u32[]{:S(2)}, u32[]{:S(2)}) collective-permute-start(bf16[3,224,512]{2,1,0:T(8,128)(2,1)} %collective-permute-done.1.refs_0_), channel_id=1, source_target_pairs={{0,1},{1,0},{2,3},{3,2},{4,5},{5,4},{6,7},{7,6}} | collective-permute-start | bytes 2064392 | tf_op jit(solution)/shard_map/ppermute | solution.py:389
  387.3 10.8 %collective-permute-start = (bf16[3,224,256]{2,1,0:T(8,128)(2,1)}, bf16[3,224,256]{2,1,0:T(8,128)(2,1)}, u32[]{:S(2)}, u32[]{:S(2)}) collective-permute-start(bf16[3,224,256]{2,1,0:T(8,128)(2,1)} %get-tuple-element.177), channel_id=1, source_target_pairs={{0,2},{2,0},{1,3},{3,1},{4,6},{6,4},{5,7},{7,5}} | collective-permute-start | bytes 1032200 | tf_op jit(solution)/shard_map/ppermute | solution.py:382
  392.5 0.8 copy-start.4
  398.1 3.7 collective-permute-start.10
  401.8 0.7 copy-start.5
